TPU v7x, 32 devices: a whole 2x2x4 slice. The times are simulated.
32 devices in a mesh: dp: 8 (over y, x, core), space: 4 (over z).
Axes of the slice: x: 2, y: 2, z: 4, core: 2. Of those that a mesh axis runs over, the one named last changes fastest.
Arguments:
- act_in: bfloat16 [8, 8, 64, 2048], P('dp', 'space'), may hold values from -6 to 6
- weight_one: bfloat16 [3, 3, 3, 32, 64], replicated, may hold values from -0.21875 to 0.21875
- bias_one: float32 [64], replicated, may hold values from -3 to 3
- weight_two: bfloat16 [3, 3, 3, 64, 128], replicated, may hold values from -0.15625 to 0.15625
- bias_two: float32 [128], replicated, may hold values from -3 to 3
- cotangent: bfloat16 [8, 4, 32, 4096], P('dp', 'space'), may hold values from -24 to 24
Outputs:
- grad_input: bfloat16 [8, 8, 64, 2048], P('dp', 'space')
- grad_w_one: float32 [3, 3, 3, 32, 64], replicated
- grad_b_one: float32 [64], replicated
- grad_w_two: float32 [3, 3, 3, 64, 128], replicated
- grad_b_two: float32 [128], replicated
All inputs are finite; a program needn't handle non-finite values.
Results may differ from a plain program's by a relative error of at most 0.01.
Values may be sent and summed in bfloat16 or wider, within the bound.
A program may use at most 128 MiB of HBM per device.

v0:
```python
import functools
import math

import jax
import jax.numpy as jnp
from jax import lax
from jax.experimental import pallas as pl
from jax.experimental.pallas import tpu as pltpu
from jax.sharding import PartitionSpec as P

MESH = pl.DeviceIdType.MESH
F32 = jnp.float32
BF16 = jnp.bfloat16


def dot(a, b):
    return lax.dot_general(a, b, (((1,), (0,)), ((), ())), preferred_element_type=F32)


def dot_t(a, b):
    return lax.dot_general(a, b, (((1,), (1,)), ((), ())), preferred_element_type=F32)


def sigmoid(x):
    return 0.5 * jnp.tanh(0.5 * x) + 0.5


def slope(x):
    s = sigmoid(x)
    return s * (1.0 + x * (1.0 - s))


def lanes(shape):
    return lax.broadcasted_iota(jnp.int32, shape, 1)


def from_left(x, wide):
    g = lax.broadcasted_iota(jnp.int32, x.shape, 0) % wide
    return jnp.where(g == 0, 0.0, pltpu.roll(x, 1, 0))


def from_right(x, wide):
    g = lax.broadcasted_iota(jnp.int32, x.shape, 0) % wide
    return jnp.where(g == wide - 1, 0.0, pltpu.roll(x, x.shape[0] - 1, 0))


def edge_lanes(x, wide):
    return jnp.where(lanes(x.shape) < 64, from_right(x, wide), from_left(x, wide))


class Sum:
    def __init__(self, n, m, me, my, each, x, got, part, gots, out, acc, sems):
        self.n, self.m, self.me, self.my, self.each = n, m, me, my, each
        self.x, self.got, self.part, self.gots, self.out, self.acc = x, got, part, gots, out, acc
        self.send, self.recv, self.send_s, self.recv_s = sems

    def rows(self, count, start):
        return pl.ds(pl.multiple_of(start * self.each, 16), count * self.each)

    def to_dp(self, k, src, dst, base):
        return pltpu.make_async_remote_copy(
            src_ref=src,
            dst_ref=dst,
            send_sem=self.send.at[base + k],
            recv_sem=self.recv.at[base + k],
            device_id=(lax.rem(self.me + k, self.n), self.my),
            device_id_type=MESH,
        )

    def to_space(self, k, src, dst, base):
        return pltpu.make_async_remote_copy(
            src_ref=src,
            dst_ref=dst,
            send_sem=self.send_s.at[base + k],
            recv_sem=self.recv_s.at[base + k],
            device_id=(self.me, lax.rem(self.my + k, self.m)),
            device_id_type=MESH,
        )

    def step1(self):
        n, m = self.n, self.m
        self.c1 = []
        for k in range(1, n):
            src = self.x.at[self.rows(m, lax.rem(self.me + k, n) * m)]
            self.c1.append(self.to_dp(k, src, self.got.at[k], 0))
        for c in self.c1:
            c.start()

    def step2(self):
        n, m, each = self.n, self.m, self.each
        for c in self.c1:
            c.wait_recv()
        total = self.x[self.rows(m, self.me * m), :].astype(F32)
        for k in range(1, n):
            total = total + self.got[k].astype(F32)
        self.acc[...] = total
        self.part[...] = total.astype(BF16)
        self.c2 = []
        for k in range(1, m):
            src = self.part.at[self.rows(1, lax.rem(self.my + k, m))]
            self.c2.append(self.to_space(k, src, self.gots.at[k], 0))
        for c in self.c2:
            c.start()
        for c in self.c1:
            c.wait_send()

    def step3(self):
        m = self.m
        for c in self.c2:
            c.wait_recv()
        total = self.acc[self.rows(1, self.my), :]
        for k in range(1, m):
            total = total + self.gots[k].astype(F32)
        mine = self.rows(1, self.me * m + self.my)
        self.out[mine, :] = total.astype(BF16)
        self.c3 = [self.to_space(k, self.out.at[mine], self.out.at[mine], m) for k in range(1, m)]
        for c in self.c3:
            c.start()
        for c in self.c2:
            c.wait_send()

    def step4(self):
        n, m = self.n, self.m
        for c in self.c3:
            c.wait_recv()
        mine = self.rows(m, self.me * m)
        self.c4 = [self.to_dp(k, self.out.at[mine], self.out.at[mine], n) for k in range(1, n)]
        for c in self.c4:
            c.start()
        for c in self.c3:
            c.wait_send()

    def step5(self):
        for c in self.c4:
            c.wait_recv()
        for c in self.c4:
            c.wait_send()


def kernel(
    n, m, scale_one, scale_two, each1, each2,
    act, w1, b1, w2, b2, cot,
    gin, gw1, gb1, gw2, gb2,
    xr, x2, pre1, pool, p2, pre2, cotr, d2, d2t, gp, d1, d1t, gx,
    k1, k2, g1, g2, b1s, b2s, gb1s, gb2s, fold1,
    acth, poolh, gps, gpr, gxs, gxr,
    s2x, s2got, s2part, s2gots, s2out, s2acc,
    s1x, s1got, s1part, s1gots, s1out, s1acc,
    hsend, hrecv, dsend2, drecv2, zsend2, zrecv2, dsend1, drecv1, zsend1, zrecv1,
):
    me = lax.axis_index("dp")
    my = lax.axis_index("space")
    slab, side, merged = act.shape[1:]
    wide = merged // 128
    slab2, half = cot.shape[1:3]
    rows, rows2 = side * wide, half * wide
    chan_in, chan_mid = w1.shape[1:]
    chan_out = w2.shape[2]
    big = min(512, rows2)
    small = 256

    barrier = pltpu.get_barrier_semaphore()
    for k in range(1, n):
        pl.semaphore_signal(barrier, inc=1, device_id=(lax.rem(me + k, n), my), device_id_type=MESH)
    for k in range(1, m):
        pl.semaphore_signal(barrier, inc=1, device_id=(me, lax.rem(my + k, m)), device_id_type=MESH)

    def loop(count, body):
        if count == 1:
            body(0)
        else:
            lax.fori_loop(0, count, lambda i, c: (body(i), c)[1], 0)

    def at(i, size, shift=0):
        return pl.ds(pl.multiple_of(i * size + shift, 16), size)

    def down(e, src, dst):
        return pltpu.make_async_remote_copy(
            src_ref=src, dst_ref=dst.at[1], send_sem=hsend.at[2 * e], recv_sem=hrecv.at[2 * e],
            device_id=(me, jnp.maximum(my - 1, 0)), device_id_type=MESH,
        )

    def up(e, src, dst):
        return pltpu.make_async_remote_copy(
            src_ref=src, dst_ref=dst.at[0], send_sem=hsend.at[2 * e + 1], recv_sem=hrecv.at[2 * e + 1],
            device_id=(me, jnp.minimum(my + 1, m - 1)), device_id_type=MESH,
        )

    def send_halo(e, first, last, dst):
        @pl.when(my > 0)
        def _():
            down(e, first, dst).start()

        @pl.when(my < m - 1)
        def _():
            up(e, last, dst).start()

    def wait_halo(e, first, last, dst):
        @pl.when(my > 0)
        def _():
            up(e, last, dst).wait_recv()
            down(e, first, dst).wait_send()

        @pl.when(my < m - 1)
        def _():
            down(e, first, dst).wait_recv()
            up(e, last, dst).wait_send()

        @pl.when(my == 0)
        def _():
            dst[0] = jnp.zeros(dst.shape[1:], dst.dtype)

        @pl.when(my == m - 1)
        def _():
            dst[1] = jnp.zeros(dst.shape[1:], dst.dtype)

    k1[...] = jnp.zeros(k1.shape, BF16)
    for k in range(3):
        for j in range(3):
            for i in range(3):
                tap = w1[(k * 3 + j) * 3 + i]
                for b in range(4):
                    row = ((b + i - 1) * chan_in) % 256 + (k * 3 + j) * 256
                    k1[row : row + chan_in, b * chan_mid : (b + 1) * chan_mid] = tap

    for b in range(4):
        b1s[0:1, b * chan_mid : (b + 1) * chan_mid] = b1[...]
    for b in range(2):
        b2s[0:1, b * chan_out : (b + 1) * chan_out] = b2[...]

    pl.semaphore_wait(barrier, n + m - 2)
    send_halo(0, act.at[0, 0], act.at[0, slab - 1], acth)

    def clear_edges(ref, planes, count):
        for d in range(planes):
            ref[d, 0:wide, :] = jnp.zeros((wide, ref.shape[2]), BF16)
            ref[d, count + wide : count + 2 * wide, :] = jnp.zeros((wide, ref.shape[2]), BF16)

    clear_edges(x2, slab + 2, rows)
    clear_edges(p2, slab2 + 2, rows2)
    clear_edges(d2, slab2, rows2)
    clear_edges(d1, slab, rows)

    def load_plane(src, d):
        for g in range(wide):
            xr[pl.ds(g, side, stride=wide), :] = src[:, g * 128 : (g + 1) * 128].astype(F32)

        def body(r):
            main = xr[at(r, small), :]
            x2[d, at(r, small, wide), 0:128] = main.astype(BF16)
            x2[d, at(r, small, wide), 128:256] = edge_lanes(main, wide).astype(BF16)

        loop(rows // small, body)

    for d in range(slab):
        load_plane(act.at[0, d], d + 1)

    def taps(ref, planes, r, size, shifts):
        return jnp.concatenate([ref[p, at(r, size, s * wide), :] for p in planes for s in shifts], axis=1)

    for d in range(slab):
        ks = [k for k in range(3) if 0 <= d + k - 1 < slab]

        def body(r, d=d, ks=ks):
            left = taps(x2, [d + k for k in ks], r, big, (0, 1, 2))
            pre1[d, at(r, big), :] = dot(left, k1[ks[0] * 768 : (ks[-1] + 1) * 768, :])

        loop(rows // big, body)

    k2[...] = jnp.zeros(k2.shape, BF16)
    for k in range(3):
        for j in range(3):
            for i in range(3):
                tap = w2[(k * 3 + j) * 3 + i]
                for b in range(2):
                    row = ((b + i - 1) * chan_mid) % 256 + (k * 3 + j) * 256
                    k2[row : row + chan_mid, b * chan_out : (b + 1) * chan_out] = tap
    for d in range(slab2):
        for g in range(wide):
            for t in range(2):
                cotr[d, t, pl.ds(g, half, stride=wide), :] = cot[0, d, :, g * 256 + t * 128 : g * 256 + t * 128 + 128].astype(F32)

    wait_halo(0, act.at[0, 0], act.at[0, slab - 1], acth)
    load_plane(acth.at[0], 0)
    load_plane(acth.at[1], slab + 1)

    def put_pooled(d, r, size, main):
        p2[d, at(r, size, wide), 0:128] = main.astype(BF16)
        p2[d, at(r, size, wide), 128:256] = edge_lanes(main, wide).astype(BF16)

    for e in range(slab2):

        def body(r, e=e):
            total = None
            for d in (2 * e, 2 * e + 1):
                pre = pre1[d, at(r, big), :] + b1s[0:1, :]
                if d == 0:
                    pre = pre + dot(taps(x2, [0], r, big, (0, 1, 2)), k1[0:768, :])
                if d == slab - 1:
                    pre = pre + dot(taps(x2, [slab + 1], r, big, (0, 1, 2)), k1[1536:2304, :])
                pre1[d, at(r, big), :] = pre
                one = pre * sigmoid(pre)
                total = one if total is None else total + one
            pairs = total.reshape(big // (2 * wide), 2, wide, 256)
            quad = (pairs[:, 0] + pairs[:, 1]).reshape(big // 2, 256)
            a, b = quad[:, 0:128], quad[:, 128:256]
            a = a + pltpu.roll(a, 64, 1)
            b = b + pltpu.roll(b, 64, 1)
            mean = (jnp.where(lanes(a.shape) < 64, a, b) * 0.125).astype(BF16)
            pool[e, at(r, big // 2), :] = mean
            put_pooled(e + 1, r, big // 2, mean.astype(F32))

        loop(rows // big, body)

    send_halo(1, pool.at[0], pool.at[slab2 - 1], poolh)

    for e in range(slab2):
        ks = [k for k in range(3) if 0 <= e + k - 1 < slab2]

        def body(r, e=e, ks=ks):
            left = taps(p2, [e + k for k in ks], r, big, (0, 1, 2))
            pre2[e, at(r, big), :] = dot(left, k2[ks[0] * 768 : (ks[-1] + 1) * 768, :])

        loop(rows2 // big, body)

    g2[...] = jnp.zeros(g2.shape, BF16)
    g1[...] = jnp.zeros(g1.shape, BF16)
    for k in range(3):
        for j in range(3):
            for i in range(3):
                tap = w2[(k * 3 + j) * 3 + i]
                for b in range(2):
                    lane = j * 512 + ((b - i + 1) * chan_out) % 512
                    g2[k * 128 + b * chan_mid : k * 128 + (b + 1) * chan_mid, lane : lane + chan_out] = tap
                tap = w1[(k * 3 + j) * 3 + i]
                for b in range(4):
                    lane = j * 384 + ((b - i + 1) * chan_mid) % 384
                    g1[k * 128 + b * chan_in : k * 128 + (b + 1) * chan_in, lane : lane + chan_mid] = tap

    wait_halo(1, pool.at[0], pool.at[slab2 - 1], poolh)
    for q, d in ((0, 0), (1, slab2 + 1)):

        def body(r, q=q, d=d):
            put_pooled(d, r, small, poolh[q, at(r, small), :].astype(F32))

        loop(rows2 // small, body)

    def col_sum(x):
        return x.reshape(x.shape[0] // 8, 8, x.shape[1]).sum(axis=0)

    gb2s[...] = jnp.zeros(gb2s.shape, F32)
    gb1s[...] = jnp.zeros(gb1s.shape, F32)
    for e in range(slab2):

        def body(r, e=e):
            pre = pre2[e, at(r, big), :] + b2s[0:1, :]
            if e == 0:
                pre = pre + dot(taps(p2, [0], r, big, (0, 1, 2)), k2[0:768, :])
            if e == slab2 - 1:
                pre = pre + dot(taps(p2, [slab2 + 1], r, big, (0, 1, 2)), k2[1536:2304, :])
            cots = jnp.concatenate([cotr[e, 0, at(r, big), :], cotr[e, 1, at(r, big), :]], axis=1)
            delta = cots * slope(pre)
            low = delta.astype(BF16)
            d2[e, at(r, big, wide), 0:256] = low
            d2[e, at(r, big, wide), 256:384] = from_right(delta[:, 0:128], wide).astype(BF16)
            d2[e, at(r, big, wide), 384:512] = from_left(delta[:, 128:256], wide).astype(BF16)
            rounded = low.astype(F32)
            gb2s[...] += col_sum(rounded)
            pre2[e, at(r, big), :] = rounded

        loop(rows2 // big, body)
        d2t[:, e * rows2 : (e + 1) * rows2] = pre2[e].T.astype(BF16)

    for e in range(slab2):

        def body(r, e=e):
            out = dot_t(taps(d2, [e], r, big, (2, 1, 0)), g2[...])
            for k in range(3):
                part = out[:, k * 128 : (k + 1) * 128]
                first = k == 2 or e == 0
                gp[e + k, at(r, big), :] = part if first else gp[e + k, at(r, big), :] + part

        loop(rows2 // big, body)

    gps[0] = gp[0].astype(BF16)
    gps[1] = gp[slab2 + 1].astype(BF16)
    send_halo(2, gps.at[0], gps.at[1], gpr)

    for k in range(3):
        for j in range(3):
            acc = None
            for e in range(slab2):
                one = dot(d2t[:, e * rows2 : (e + 1) * rows2], p2[e + k, j * wide : j * wide + rows2, :])
                acc = one if acc is None else acc + one
            t0, t1 = pltpu.roll(acc[0:128, 0:128], 64, 1), pltpu.roll(acc[0:128, 128:256], 64, 1)
            low = lanes(t0.shape) < 64
            f0 = jnp.where(low, t1, t0) + acc[128:256, 0:128]
            f1 = jnp.where(low, t0, t1) + acc[128:256, 128:256]
            base = (k * 3 + j) * 192
            s2x[base : base + 128, :] = f0.T.astype(BF16)
            s2x[base + 128 : base + 192, :] = f1.T[0:64, :].astype(BF16)
    bias = gb2s[...].sum(axis=0, keepdims=True)
    bias = bias[:, 0:128] + bias[:, 128:256]
    s2x[1728:1744, :] = jnp.broadcast_to(bias, (16, 128)).astype(BF16)
    if s2x.shape[0] > 1744:
        s2x[1744 : s2x.shape[0], :] = jnp.zeros((s2x.shape[0] - 1744, 128), BF16)

    sum2 = Sum(n, m, me, my, each2, s2x, s2got, s2part, s2gots, s2out, s2acc, (dsend2, drecv2, zsend2, zrecv2))
    sum1 = Sum(n, m, me, my, each1, s1x, s1got, s1part, s1gots, s1out, s1acc, (dsend1, drecv1, zsend1, zrecv1))
    sum2.step1()

    wait_halo(2, gps.at[0], gps.at[1], gpr)
    for e in range(slab2):

        def body(r, e=e):
            total = gp[e + 1, at(r, small // 2), :]
            if e == 0:
                total = total + gpr[0, at(r, small // 2), :].astype(F32)
            if e == slab2 - 1:
                total = total + gpr[1, at(r, small // 2), :].astype(F32)
            total = total * 0.125
            turned = pltpu.roll(total, 64, 1)
            low = lanes(total.shape) < 64
            both = jnp.concatenate([jnp.where(low, total, turned), jnp.where(low, turned, total)], axis=1)
            both = both.reshape(small // 2 // wide, 1, wide, 256)
            both = jnp.broadcast_to(both, (small // 2 // wide, 2, wide, 256)).reshape(small, 256)
            for d in (2 * e, 2 * e + 1):
                delta = both * slope(pre1[d, at(r, small), :])
                low_delta = delta.astype(BF16)
                d1[d, at(r, small, wide), 0:256] = low_delta
                edge = jnp.where(
                    lanes((small, 128)) < 64,
                    from_right(delta[:, 0:128], wide),
                    from_left(delta[:, 128:256], wide),
                )
                d1[d, at(r, small, wide), 256:384] = edge.astype(BF16)
                rounded = low_delta.astype(F32)
                gb1s[...] += col_sum(rounded)
                pre1[d, at(r, small), :] = rounded

        loop(rows // small, body)
    for d in range(slab):
        d1t[:, d * rows : (d + 1) * rows] = pre1[d].T.astype(BF16)
    sum2.step2()

    for k in range(3):
        for j in range(3):
            acc = None
            for d in range(slab):
                one = dot(d1t[:, d * rows : (d + 1) * rows], x2[d + k, j * wide : j * wide + rows, :])
                acc = one if acc is None else acc + one
            low = lanes((64, 128))
            total = acc[64:128, 0:128]
            total = total + jnp.where(
                low < 32, pltpu.roll(acc[0:64, 128:256], 32, 1), pltpu.roll(acc[0:64, 0:128], 32, 1)
            )
            total = total + pltpu.roll(acc[128:192, 0:128], 96, 1)
            total = total + jnp.where(
                low < 64, pltpu.roll(acc[192:256, 0:128], 64, 1), pltpu.roll(acc[192:256, 128:256], 64, 1)
            )
            t = k * 3 + j
            fold1[t % 5, (t // 5) * 64 : (t // 5) * 64 + 64, :] = total
        if k == 0:
            sum2.step3()
    fold1[4, 64:128, :] = jnp.zeros((64, 128), F32)
    for t in range(5):
        s1x[t * 96 : t * 96 + 96, :] = fold1[t].T[0:96, :].astype(BF16)
    bias = gb1s[...].sum(axis=0, keepdims=True)
    bias = bias[:, 0:128] + bias[:, 128:256]
    bias = bias + pltpu.roll(bias, 64, 1)
    s1x[480:496, :] = jnp.broadcast_to(bias, (16, 128)).astype(BF16)
    if s1x.shape[0] > 496:
        s1x[496 : s1x.shape[0], :] = jnp.zeros((s1x.shape[0] - 496, 128), BF16)
    sum1.step1()
    sum2.step4()

    for d in range(slab):

        def body(r, d=d):
            out = dot_t(taps(d1, [d], r, big, (2, 1, 0)), g1[...])
            for k in range(3):
                part = out[:, k * 128 : (k + 1) * 128]
                first = k == 2 or d == 0
                gx[d + k, at(r, big), :] = part if first else gx[d + k, at(r, big), :] + part

        loop(rows // big, body)
    gxs[0] = gx[0].astype(BF16)
    gxs[1] = gx[slab + 1].astype(BF16)
    send_halo(3, gxs.at[0], gxs.at[1], gxr)
    sum1.step2()
    sum2.step5()
    for t in range(9):
        gw2[t] = s2out[t * 192 : (t + 1) * 192, :].astype(F32) * scale_two
    gb2[...] = s2out[1728:1744, :].astype(F32)[0:1, :] * scale_two
    sum1.step3()
    wait_halo(3, gxs.at[0], gxs.at[1], gxr)
    for d in range(slab):
        total = gx[d + 1]
        if d == 0:
            total = total + gxr[0].astype(F32)
        if d == slab - 1:
            total = total + gxr[1].astype(F32)
        xr[...] = total
        for g in range(wide):
            gin[0, d, :, g * 128 : (g + 1) * 128] = xr[pl.ds(g, side, stride=wide), :].astype(BF16)
    sum1.step4()
    sum1.step5()
    for t in range(9):
        block = s1out[(t % 5) * 96 : (t % 5) * 96 + 96, :].astype(F32) * scale_one
        gw1[t] = block[:, (t // 5) * 64 : (t // 5) * 64 + 64]
    gb1[...] = s1out[480:496, :].astype(F32)[0:1, 0:64] * scale_one


def local(n, m, act_in, weight_one, bias_one, weight_two, bias_two, cotangent):
    samples, slab, side, merged = act_in.shape
    chan_in, chan_mid = weight_one.shape[3:]
    chan_out = weight_two.shape[4]
    slab2, half = cotangent.shape[1:3]
    assert samples == 1 and (chan_in, chan_mid, chan_out) == (32, 64, 128)
    scale_one = 16.0 / math.sqrt(samples * n * slab * m * side * side)
    scale_two = 1.0 / math.sqrt(samples * n * slab2 * m * half * half)
    wide = merged // 128
    rows, rows2 = side * wide, half * wide
    each = [-(-count // (n * m * 16)) * 16 for count in (496, 1744)]
    vmem = pltpu.VMEM

    def sums(size):
        return [
            vmem((n * m * size, 128), BF16),
            vmem((n, m * size, 128), BF16),
            vmem((m * size, 128), BF16),
            vmem((m, size, 128), BF16),
            vmem((n * m * size, 128), BF16),
            vmem((m * size, 128), F32),
        ]

    dma = pltpu.SemaphoreType.DMA
    spec = pl.BlockSpec(memory_space=pltpu.VMEM)
    outs = pl.pallas_call(
        functools.partial(kernel, n, m, scale_one, scale_two, each[0], each[1]),
        out_shape=[
            jax.ShapeDtypeStruct(act_in.shape, BF16),
            jax.ShapeDtypeStruct((9, 3 * chan_in, chan_mid), F32),
            jax.ShapeDtypeStruct((1, chan_mid), F32),
            jax.ShapeDtypeStruct((9, 3 * chan_mid, chan_out), F32),
            jax.ShapeDtypeStruct((1, chan_out), F32),
        ],
        in_specs=[spec] * 6,
        out_specs=[spec] * 5,
        scratch_shapes=[
            vmem((rows, 128), F32),
            vmem((slab + 2, rows + 2 * wide, 256), BF16),
            vmem((slab, rows, 256), F32),
            vmem((slab2, rows2, 128), BF16),
            vmem((slab2 + 2, rows2 + 2 * wide, 256), BF16),
            vmem((slab2, rows2, 256), F32),
            vmem((slab2, 2, rows2, 128), F32),
            vmem((slab2, rows2 + 2 * wide, 512), BF16),
            vmem((256, slab2 * rows2), BF16),
            vmem((slab2 + 2, rows2, 128), F32),
            vmem((slab, rows + 2 * wide, 384), BF16),
            vmem((256, slab * rows), BF16),
            vmem((slab + 2, rows, 128), F32),
            vmem((9 * 256, 256), BF16),
            vmem((9 * 256, 256), BF16),
            vmem((384, 3 * 384), BF16),
            vmem((384, 3 * 512), BF16),
            vmem((8, 256), F32),
            vmem((8, 256), F32),
            vmem((8, 256), F32),
            vmem((8, 256), F32),
            vmem((5, 128, 128), F32),
            vmem((2, side, merged), BF16),
            vmem((2, rows2, 128), BF16),
            vmem((2, rows2, 128), BF16),
            vmem((2, rows2, 128), BF16),
            vmem((2, rows, 128), BF16),
            vmem((2, rows, 128), BF16),
            *sums(each[1]),
            *sums(each[0]),
            dma((8,)),
            dma((8,)),
            dma((2 * n,)),
            dma((2 * n,)),
            dma((2 * m,)),
            dma((2 * m,)),
            dma((2 * n,)),
            dma((2 * n,)),
            dma((2 * m,)),
            dma((2 * m,)),
        ],
        compiler_params=pltpu.CompilerParams(
            collective_id=0, has_side_effects=True, vmem_limit_bytes=60 * 1024 * 1024
        ),
    )(
        act_in,
        weight_one.reshape(27, chan_in, chan_mid),
        bias_one.reshape(1, chan_mid),
        weight_two.reshape(27, chan_mid, chan_out),
        bias_two.reshape(1, chan_out),
        cotangent,
    )
    return (
        outs[0],
        outs[1].reshape(weight_one.shape),
        outs[2].reshape(bias_one.shape),
        outs[3].reshape(weight_two.shape),
        outs[4].reshape(bias_two.shape),
    )


def solution(mesh):
    placed = (P("dp", "space", None, None), P(), P(), P(), P(), P("dp", "space", None, None))
    return jax.shard_map(
        functools.partial(local, mesh.shape["dp"], mesh.shape["space"]),
        mesh=mesh,
        in_specs=placed,
        out_specs=(P("dp", "space", None, None), P(), P(), P(), P()),
        check_vma=False,
    )
```

profile of v0, /device:TPU:0, one launch (start us, length us, event | category | flops | bytes accessed | tf_op | source)
XLA Modules:
  0.0 65.1 jit_solution(6053691307524215729)
XLA Ops:
  0.6 59.7 %shard_map.101 = (bf16[1,2,64,2048]{3,2,1,0:T(8,128)(2,1)}, f32[9,96,64]{2,1,0:T(8,128)}, f32[1,64]{1,0:T(1,128)}, f32[9,192,128]{2,1,0:T(8,128)}, f32[1,128]{1,0:T(1,128)}) custom-call(bf16[1,2,64,2048]{3,2,1,0:T(8,128)(2,1)} %act.1, bf16[27,32,64]{2,1,0:T(8,128)(2,1)} %bitcast.11, f32[1,64]{1,0:T(1,128)} %bitcast.12, bf16[27,64,128]{2,1,0:T(8,128)(2,1)} %bitcast.9, ...), custom_call_target="tpu_custom_call" | custom-call | tf_op jit(solution)/shard_map/pallas_call | solution.py:539
  60.3 0.0 copy-start.1
  60.4 0.0 copy-start
  60.4 2.0 %copy.16 = bf16[1,2,64,2048]{3,2,1,0:T(8,128)(2,1)} copy(bf16[1,2,64,2048]{3,2,1,0:T(8,128)(2,1)} %get-tuple-element.20) | data formatting | bytes 1048576
  62.3 0.0 copy-done.1
  62.3 0.0 copy-start.3
  62.4 0.8 %copy.17 = f32[3,3,3,32,64]{4,3,2,1,0:T(8,128)} copy(f32[3,3,3,32,64]{4,3,2,1,0:T(8,128)S(1)} %bitcast.10) | data formatting | bytes 442368
  63.1 0.0 copy-done.3
  63.1 0.5 copy.18
  63.6 0.0 copy-done
  63.6 0.0 copy-start.2
  63.6 0.9 %copy.19 = f32[3,3,3,64,128]{4,3,2,1,0:T(8,128)} copy(f32[3,3,3,64,128]{4,3,2,1,0:T(8,128)S(1)} %bitcast.8) | data formatting | bytes 1769472
  64.5 0.0 copy-done.2
  64.5 0.5 copy.20
Async XLA Ops:
  60.3 2.0 %copy-start.1 = (f32[9,96,64]{2,1,0:T(8,128)S(1)}, f32[9,96,64]{2,1,0:T(8,128)}, u32[]{:S(2)}) copy-start(f32[9,96,64]{2,1,0:T(8,128)} %get-tuple-element.11) | copy-start | bytes 663556
  60.4 3.3 %copy-start = (f32[9,192,128]{2,1,0:T(8,128)S(1)}, f32[9,192,128]{2,1,0:T(8,128)}, u32[]{:S(2)}) copy-start(f32[9,192,128]{2,1,0:T(8,128)} %get-tuple-element.13) | copy-start | bytes 2654212
  62.3 0.8 %copy-start.3 = (f32[1,64]{1,0:T(1,128)S(1)}, f32[1,64]{1,0:T(1,128)}, u32[]{:S(2)}) copy-start(f32[1,64]{1,0:T(1,128)} %get-tuple-element.12) | copy-start | bytes 772
  63.6 0.9 %copy-start.2 = (f32[1,128]{1,0:T(1,128)S(1)}, f32[1,128]{1,0:T(1,128)}, u32[]{:S(2)}) copy-start(f32[1,128]{1,0:T(1,128)} %get-tuple-element.14) | copy-start | bytes 1540
where the time goes:
time: 65.2 us; the launch traced here: 65.1 us
  Pallas kernels  59.7 us (92%)
  local copies, waits for them, and re-layouts  4.7 us (7%)
  between operations  0.66 us (1%)
    pallas_call x1, Pallas kernels, local(): pl.pallas_call(functools.partial(kernel, n, m, scale_one, scale_two, each...  59.7 us
    unnamed x13, local copies, waits for them, and re-layouts  4.7 us

commit v1 on v0

--- a/solution.py
+++ b/solution.py
@@ -134,6 +134,39 @@
         for c in self.c4:
             c.wait_recv()
         for c in self.c4:
+            c.wait_send()
+
+
+class ShortSum(Sum):
+    def step2(self):
+        n, m = self.n, self.m
+        for c in self.c1:
+            c.wait_recv()
+        total = self.x[self.rows(m, self.me * m), :].astype(F32)
+        for k in range(1, n):
+            total = total + self.got[k].astype(F32)
+        low = total.astype(BF16)
+        self.part[...] = low
+        self.gots[self.my] = low
+        self.c2 = [self.to_space(k, self.part, self.gots.at[self.my], 0) for k in range(1, m)]
+        for c in self.c2:
+            c.start()
+        for c in self.c1:
+            c.wait_send()
+
+    def step3(self):
+        n, m = self.n, self.m
+        for c in self.c2:
+            c.wait_recv()
+        total = self.gots[0].astype(F32)
+        for k in range(1, m):
+            total = total + self.gots[k].astype(F32)
+        mine = self.rows(m, self.me * m)
+        self.out[mine, :] = total.astype(BF16)
+        self.c4 = [self.to_dp(k, self.out.at[mine], self.out.at[mine], n) for k in range(1, n)]
+        for c in self.c4:
+            c.start()
+        for c in self.c2:
             c.wait_send()
 
 
@@ -174,45 +207,68 @@
     def at(i, size, shift=0):
         return pl.ds(pl.multiple_of(i * size + shift, 16), size)
 
-    def down(e, src, dst):
+    def down(e, first, above):
         return pltpu.make_async_remote_copy(
-            src_ref=src, dst_ref=dst.at[1], send_sem=hsend.at[2 * e], recv_sem=hrecv.at[2 * e],
+            src_ref=first, dst_ref=above, send_sem=hsend.at[2 * e], recv_sem=hrecv.at[2 * e],
             device_id=(me, jnp.maximum(my - 1, 0)), device_id_type=MESH,
         )
 
-    def up(e, src, dst):
+    def up(e, last, below):
         return pltpu.make_async_remote_copy(
-            src_ref=src, dst_ref=dst.at[0], send_sem=hsend.at[2 * e + 1], recv_sem=hrecv.at[2 * e + 1],
+            src_ref=last, dst_ref=below, send_sem=hsend.at[2 * e + 1], recv_sem=hrecv.at[2 * e + 1],
             device_id=(me, jnp.minimum(my + 1, m - 1)), device_id_type=MESH,
         )
 
-    def send_halo(e, first, last, dst):
+    def send_down(e, first, last, below, above):
         @pl.when(my > 0)
         def _():
-            down(e, first, dst).start()
-
+            down(e, first, above).start()
+
+    def send_up(e, first, last, below, above):
         @pl.when(my < m - 1)
         def _():
-            up(e, last, dst).start()
-
-    def wait_halo(e, first, last, dst):
+            up(e, last, below).start()
+
+    def send_halo(e, *refs):
+        send_down(e, *refs)
+        send_up(e, *refs)
+
+    def wait_halo(e, first, last, below, above):
         @pl.when(my > 0)
         def _():
-            up(e, last, dst).wait_recv()
-            down(e, first, dst).wait_send()
+            up(e, last, below).wait_recv()
+            down(e, first, above).wait_send()
 
         @pl.when(my < m - 1)
         def _():
-            down(e, first, dst).wait_recv()
-            up(e, last, dst).wait_send()
+            down(e, first, above).wait_recv()
+            up(e, last, below).wait_send()
 
         @pl.when(my == 0)
         def _():
-            dst[0] = jnp.zeros(dst.shape[1:], dst.dtype)
+            below[...] = jnp.zeros(below.shape, below.dtype)
 
         @pl.when(my == m - 1)
         def _():
-            dst[1] = jnp.zeros(dst.shape[1:], dst.dtype)
+            above[...] = jnp.zeros(above.shape, above.dtype)
+
+    cuts = (0, side * 3 // 4, side)
+
+    def act_halo(c):
+        part = pl.ds(cuts[c], cuts[c + 1] - cuts[c])
+        return act.at[0, 0, part], act.at[0, slab - 1, part], acth.at[0, part], acth.at[1, part]
+
+    def half_halo(c, first, last, got):
+        part = pl.ds(c * (rows2 // 2), rows2 // 2)
+        return first.at[part], last.at[part], got.at[0, part], got.at[1, part]
+
+    def pool_halo(c):
+        return half_halo(c, pool.at[0], pool.at[slab2 - 1], poolh)
+
+    def gp_halo(c):
+        return half_halo(c, gps.at[0], gps.at[1], gpr)
+
+    gx_halo = (gxs.at[0], gxs.at[1], gxr.at[0], gxr.at[1])
 
     k1[...] = jnp.zeros(k1.shape, BF16)
     for k in range(3):
@@ -229,7 +285,8 @@
         b2s[0:1, b * chan_out : (b + 1) * chan_out] = b2[...]
 
     pl.semaphore_wait(barrier, n + m - 2)
-    send_halo(0, act.at[0, 0], act.at[0, slab - 1], acth)
+    for c in range(2):
+        send_halo(c, *act_halo(c))
 
     def clear_edges(ref, planes, count):
         for d in range(planes):
@@ -241,19 +298,21 @@
     clear_edges(d2, slab2, rows2)
     clear_edges(d1, slab, rows)
 
-    def load_plane(src, d):
+    def load_plane(src, d, start, stop):
         for g in range(wide):
-            xr[pl.ds(g, side, stride=wide), :] = src[:, g * 128 : (g + 1) * 128].astype(F32)
+            to = pl.ds(start * wide + g, stop - start, stride=wide)
+            xr[to, :] = src[start:stop, g * 128 : (g + 1) * 128].astype(F32)
+        skip = start * wide
 
         def body(r):
-            main = xr[at(r, small), :]
-            x2[d, at(r, small, wide), 0:128] = main.astype(BF16)
-            x2[d, at(r, small, wide), 128:256] = edge_lanes(main, wide).astype(BF16)
-
-        loop(rows // small, body)
+            main = xr[at(r, small, skip), :]
+            x2[d, at(r, small, skip + wide), 0:128] = main.astype(BF16)
+            x2[d, at(r, small, skip + wide), 128:256] = edge_lanes(main, wide).astype(BF16)
+
+        loop((stop - start) * wide // small, body)
 
     for d in range(slab):
-        load_plane(act.at[0, d], d + 1)
+        load_plane(act.at[0, d], d + 1, 0, side)
 
     def taps(ref, planes, r, size, shifts):
         return jnp.concatenate([ref[p, at(r, size, s * wide), :] for p in planes for s in shifts], axis=1)
@@ -280,39 +339,39 @@
             for t in range(2):
                 cotr[d, t, pl.ds(g, half, stride=wide), :] = cot[0, d, :, g * 256 + t * 128 : g * 256 + t * 128 + 128].astype(F32)
 
-    wait_halo(0, act.at[0, 0], act.at[0, slab - 1], acth)
-    load_plane(acth.at[0], 0)
-    load_plane(acth.at[1], slab + 1)
-
     def put_pooled(d, r, size, main):
         p2[d, at(r, size, wide), 0:128] = main.astype(BF16)
         p2[d, at(r, size, wide), 128:256] = edge_lanes(main, wide).astype(BF16)
 
-    for e in range(slab2):
-
-        def body(r, e=e):
-            total = None
-            for d in (2 * e, 2 * e + 1):
-                pre = pre1[d, at(r, big), :] + b1s[0:1, :]
-                if d == 0:
-                    pre = pre + dot(taps(x2, [0], r, big, (0, 1, 2)), k1[0:768, :])
-                if d == slab - 1:
-                    pre = pre + dot(taps(x2, [slab + 1], r, big, (0, 1, 2)), k1[1536:2304, :])
-                pre1[d, at(r, big), :] = pre
-                one = pre * sigmoid(pre)
-                total = one if total is None else total + one
-            pairs = total.reshape(big // (2 * wide), 2, wide, 256)
-            quad = (pairs[:, 0] + pairs[:, 1]).reshape(big // 2, 256)
-            a, b = quad[:, 0:128], quad[:, 128:256]
-            a = a + pltpu.roll(a, 64, 1)
-            b = b + pltpu.roll(b, 64, 1)
-            mean = (jnp.where(lanes(a.shape) < 64, a, b) * 0.125).astype(BF16)
-            pool[e, at(r, big // 2), :] = mean
-            put_pooled(e + 1, r, big // 2, mean.astype(F32))
-
-        loop(rows // big, body)
-
-    send_halo(1, pool.at[0], pool.at[slab2 - 1], poolh)
+    for part in range(2):
+        wait_halo(part, *act_halo(part))
+        load_plane(acth.at[0], 0, cuts[part], cuts[part + 1])
+        load_plane(acth.at[1], slab + 1, cuts[part], cuts[part + 1])
+        for e in range(slab2):
+
+            def body(r, e=e, part=part):
+                r = r + part * (rows // 2 // big)
+                total = None
+                for d in (2 * e, 2 * e + 1):
+                    pre = pre1[d, at(r, big), :] + b1s[0:1, :]
+                    if d == 0:
+                        pre = pre + dot(taps(x2, [0], r, big, (0, 1, 2)), k1[0:768, :])
+                    if d == slab - 1:
+                        pre = pre + dot(taps(x2, [slab + 1], r, big, (0, 1, 2)), k1[1536:2304, :])
+                    pre1[d, at(r, big), :] = pre
+                    one = pre * sigmoid(pre)
+                    total = one if total is None else total + one
+                pairs = total.reshape(big // (2 * wide), 2, wide, 256)
+                quad = (pairs[:, 0] + pairs[:, 1]).reshape(big // 2, 256)
+                a, b = quad[:, 0:128], quad[:, 128:256]
+                a = a + pltpu.roll(a, 64, 1)
+                b = b + pltpu.roll(b, 64, 1)
+                mean = (jnp.where(lanes(a.shape) < 64, a, b) * 0.125).astype(BF16)
+                pool[e, at(r, big // 2), :] = mean
+                put_pooled(e + 1, r, big // 2, mean.astype(F32))
+
+            loop(rows // 2 // big, body)
+        send_halo(2 + part, *pool_halo(part))
 
     for e in range(slab2):
         ks = [k for k in range(3) if 0 <= e + k - 1 < slab2]
@@ -337,7 +396,8 @@
                     lane = j * 384 + ((b - i + 1) * chan_mid) % 384
                     g1[k * 128 + b * chan_in : k * 128 + (b + 1) * chan_in, lane : lane + chan_mid] = tap
 
-    wait_halo(1, pool.at[0], pool.at[slab2 - 1], poolh)
+    for c in range(2):
+        wait_halo(2 + c, *pool_halo(c))
     for q, d in ((0, 0), (1, slab2 + 1)):
 
         def body(r, q=q, d=d):
@@ -384,7 +444,8 @@
 
     gps[0] = gp[0].astype(BF16)
     gps[1] = gp[slab2 + 1].astype(BF16)
-    send_halo(2, gps.at[0], gps.at[1], gpr)
+    for c in range(2):
+        send_halo(4 + c, *gp_halo(c))
 
     for k in range(3):
         for j in range(3):
@@ -406,41 +467,57 @@
         s2x[1744 : s2x.shape[0], :] = jnp.zeros((s2x.shape[0] - 1744, 128), BF16)
 
     sum2 = Sum(n, m, me, my, each2, s2x, s2got, s2part, s2gots, s2out, s2acc, (dsend2, drecv2, zsend2, zrecv2))
-    sum1 = Sum(n, m, me, my, each1, s1x, s1got, s1part, s1gots, s1out, s1acc, (dsend1, drecv1, zsend1, zrecv1))
+    sum1 = ShortSum(n, m, me, my, each1, s1x, s1got, s1part, s1gots, s1out, s1acc, (dsend1, drecv1, zsend1, zrecv1))
     sum2.step1()
 
-    wait_halo(2, gps.at[0], gps.at[1], gpr)
-    for e in range(slab2):
-
-        def body(r, e=e):
-            total = gp[e + 1, at(r, small // 2), :]
-            if e == 0:
-                total = total + gpr[0, at(r, small // 2), :].astype(F32)
-            if e == slab2 - 1:
-                total = total + gpr[1, at(r, small // 2), :].astype(F32)
-            total = total * 0.125
-            turned = pltpu.roll(total, 64, 1)
-            low = lanes(total.shape) < 64
-            both = jnp.concatenate([jnp.where(low, total, turned), jnp.where(low, turned, total)], axis=1)
-            both = both.reshape(small // 2 // wide, 1, wide, 256)
-            both = jnp.broadcast_to(both, (small // 2 // wide, 2, wide, 256)).reshape(small, 256)
-            for d in (2 * e, 2 * e + 1):
-                delta = both * slope(pre1[d, at(r, small), :])
-                low_delta = delta.astype(BF16)
-                d1[d, at(r, small, wide), 0:256] = low_delta
-                edge = jnp.where(
-                    lanes((small, 128)) < 64,
-                    from_right(delta[:, 0:128], wide),
-                    from_left(delta[:, 128:256], wide),
-                )
-                d1[d, at(r, small, wide), 256:384] = edge.astype(BF16)
-                rounded = low_delta.astype(F32)
-                gb1s[...] += col_sum(rounded)
-                pre1[d, at(r, small), :] = rounded
-
-        loop(rows // small, body)
+    for c in range(2):
+        wait_halo(4 + c, *gp_halo(c))
+        for e in range(slab2):
+
+            def body(r, e=e, c=c):
+                r = r + c * (rows // 2 // small)
+                total = gp[e + 1, at(r, small // 2), :]
+                if e == 0:
+                    total = total + gpr[0, at(r, small // 2), :].astype(F32)
+                if e == slab2 - 1:
+                    total = total + gpr[1, at(r, small // 2), :].astype(F32)
+                total = total * 0.125
+                turned = pltpu.roll(total, 64, 1)
+                low = lanes(total.shape) < 64
+                both = jnp.concatenate([jnp.where(low, total, turned), jnp.where(low, turned, total)], axis=1)
+                both = both.reshape(small // 2 // wide, 1, wide, 256)
+                both = jnp.broadcast_to(both, (small // 2 // wide, 2, wide, 256)).reshape(small, 256)
+                for d in (2 * e, 2 * e + 1):
+                    delta = both * slope(pre1[d, at(r, small), :])
+                    low_delta = delta.astype(BF16)
+                    d1[d, at(r, small, wide), 0:256] = low_delta
+                    edge = jnp.where(
+                        lanes((small, 128)) < 64,
+                        from_right(delta[:, 0:128], wide),
+                        from_left(delta[:, 128:256], wide),
+                    )
+                    d1[d, at(r, small, wide), 256:384] = edge.astype(BF16)
+                    rounded = low_delta.astype(F32)
+                    gb1s[...] += col_sum(rounded)
+                    pre1[d, at(r, small), :] = rounded
+
+            loop(rows // 2 // small, body)
     for d in range(slab):
         d1t[:, d * rows : (d + 1) * rows] = pre1[d].T.astype(BF16)
+
+    for d in range(slab):
+
+        def body(r, d=d):
+            out = dot_t(taps(d1, [d], r, big, (2, 1, 0)), g1[...])
+            for k in range(3):
+                part = out[:, k * 128 : (k + 1) * 128]
+                first = k == 2 or d == 0
+                gx[d + k, at(r, big), :] = part if first else gx[d + k, at(r, big), :] + part
+
+        loop(rows // big, body)
+        if d == 0:
+            gxs[0] = gx[0].astype(BF16)
+    gxs[1] = gx[slab + 1].astype(BF16)
     sum2.step2()
 
     for k in range(3):
@@ -460,8 +537,6 @@
             )
             t = k * 3 + j
             fold1[t % 5, (t // 5) * 64 : (t // 5) * 64 + 64, :] = total
-        if k == 0:
-            sum2.step3()
     fold1[4, 64:128, :] = jnp.zeros((64, 128), F32)
     for t in range(5):
         s1x[t * 96 : t * 96 + 96, :] = fold1[t].T[0:96, :].astype(BF16)
@@ -472,28 +547,12 @@
     if s1x.shape[0] > 496:
         s1x[496 : s1x.shape[0], :] = jnp.zeros((s1x.shape[0] - 496, 128), BF16)
     sum1.step1()
+    sum2.step3()
+    send_halo(6, *gx_halo)
     sum2.step4()
-
-    for d in range(slab):
-
-        def body(r, d=d):
-            out = dot_t(taps(d1, [d], r, big, (2, 1, 0)), g1[...])
-            for k in range(3):
-                part = out[:, k * 128 : (k + 1) * 128]
-                first = k == 2 or d == 0
-                gx[d + k, at(r, big), :] = part if first else gx[d + k, at(r, big), :] + part
-
-        loop(rows // big, body)
-    gxs[0] = gx[0].astype(BF16)
-    gxs[1] = gx[slab + 1].astype(BF16)
-    send_halo(3, gxs.at[0], gxs.at[1], gxr)
     sum1.step2()
-    sum2.step5()
-    for t in range(9):
-        gw2[t] = s2out[t * 192 : (t + 1) * 192, :].astype(F32) * scale_two
-    gb2[...] = s2out[1728:1744, :].astype(F32)[0:1, :] * scale_two
     sum1.step3()
-    wait_halo(3, gxs.at[0], gxs.at[1], gxr)
+    wait_halo(6, *gx_halo)
     for d in range(slab):
         total = gx[d + 1]
         if d == 0:
@@ -503,7 +562,10 @@
         xr[...] = total
         for g in range(wide):
             gin[0, d, :, g * 128 : (g + 1) * 128] = xr[pl.ds(g, side, stride=wide), :].astype(BF16)
-    sum1.step4()
+    sum2.step5()
+    for t in range(9):
+        gw2[t] = s2out[t * 192 : (t + 1) * 192, :].astype(F32) * scale_two
+    gb2[...] = s2out[1728:1744, :].astype(F32)[0:1, :] * scale_two
     sum1.step5()
     for t in range(9):
         block = s1out[(t % 5) * 96 : (t % 5) * 96 + 96, :].astype(F32) * scale_one
@@ -524,12 +586,12 @@
     each = [-(-count // (n * m * 16)) * 16 for count in (496, 1744)]
     vmem = pltpu.VMEM
 
-    def sums(size):
+    def sums(size, slots):
         return [
             vmem((n * m * size, 128), BF16),
             vmem((n, m * size, 128), BF16),
             vmem((m * size, 128), BF16),
-            vmem((m, size, 128), BF16),
+            vmem((m, slots * size, 128), BF16),
             vmem((n * m * size, 128), BF16),
             vmem((m * size, 128), F32),
         ]
@@ -576,10 +638,10 @@
             vmem((2, rows2, 128), BF16),
             vmem((2, rows, 128), BF16),
             vmem((2, rows, 128), BF16),
-            *sums(each[1]),
-            *sums(each[0]),
-            dma((8,)),
-            dma((8,)),
+            *sums(each[1], 1),
+            *sums(each[0], m),
+            dma((14,)),
+            dma((14,)),
             dma((2 * n,)),
             dma((2 * n,)),
             dma((2 * m,)),

time: 65.2 us -> 53.8 us (0.83)
  Pallas kernels: 59.7 us -> 48.3 us
    pallas_call x1, Pallas kernels: 59.7 us -> 48.3 us  [local(): pl.pallas_call(functools.partial(kernel, n, m, scale_one, scale_two, each...]
where the time goes in v1:
time: 53.8 us; the launch traced here: 53.6 us
  Pallas kernels  48.3 us (90%)
  local copies, waits for them, and re-layouts  4.7 us (9%)
  between operations  0.66 us (1%)
    pallas_call x1, Pallas kernels, local(): pl.pallas_call(functools.partial(kernel, n, m, scale_one, scale_two, each...  48.3 us
    unnamed x13, local copies, waits for them, and re-layouts  4.7 us

profile of v1, /device:TPU:0, one launch (start us, length us, event | category | flops | bytes accessed | tf_op | source)
XLA Modules:
  0.0 53.6 jit_solution(11093107360852453230)
XLA Ops:
  0.6 48.3 %shard_map.101 = (bf16[1,2,64,2048]{3,2,1,0:T(8,128)(2,1)}, f32[9,96,64]{2,1,0:T(8,128)}, f32[1,64]{1,0:T(1,128)}, f32[9,192,128]{2,1,0:T(8,128)}, f32[1,128]{1,0:T(1,128)}) custom-call(bf16[1,2,64,2048]{3,2,1,0:T(8,128)(2,1)} %act.1, bf16[27,32,64]{2,1,0:T(8,128)(2,1)} %bitcast.11, f32[1,64]{1,0:T(1,128)} %bitcast.12, bf16[27,64,128]{2,1,0:T(8,128)(2,1)} %bitcast.9, ...), custom_call_target="tpu_custom_call" | custom-call | tf_op jit(solution)/shard_map/pallas_call | solution.py:601
  48.9 0.0 copy-start.1
  48.9 0.0 copy-start
  49.0 2.0 %copy.16 = bf16[1,2,64,2048]{3,2,1,0:T(8,128)(2,1)} copy(bf16[1,2,64,2048]{3,2,1,0:T(8,128)(2,1)} %get-tuple-element.20) | data formatting | bytes 1048576
  50.9 0.0 copy-done.1
  50.9 0.0 copy-start.3
  50.9 0.8 %copy.17 = f32[3,3,3,32,64]{4,3,2,1,0:T(8,128)} copy(f32[3,3,3,32,64]{4,3,2,1,0:T(8,128)S(1)} %bitcast.10) | data formatting | bytes 442368
  51.7 0.0 copy-done.3
  51.7 0.5 copy.18
  52.2 0.0 copy-done
  52.2 0.0 copy-start.2
  52.2 0.9 %copy.19 = f32[3,3,3,64,128]{4,3,2,1,0:T(8,128)} copy(f32[3,3,3,64,128]{4,3,2,1,0:T(8,128)S(1)} %bitcast.8) | data formatting | bytes 1769472
  53.1 0.0 copy-done.2
  53.1 0.5 copy.20
Async XLA Ops:
  48.9 2.0 %copy-start.1 = (f32[9,96,64]{2,1,0:T(8,128)S(1)}, f32[9,96,64]{2,1,0:T(8,128)}, u32[]{:S(2)}) copy-start(f32[9,96,64]{2,1,0:T(8,128)} %get-tuple-element.11) | copy-start | bytes 663556
  48.9 3.3 %copy-start = (f32[9,192,128]{2,1,0:T(8,128)S(1)}, f32[9,192,128]{2,1,0:T(8,128)}, u32[]{:S(2)}) copy-start(f32[9,192,128]{2,1,0:T(8,128)} %get-tuple-element.13) | copy-start | bytes 2654212
  50.9 0.8 %copy-start.3 = (f32[1,64]{1,0:T(1,128)S(1)}, f32[1,64]{1,0:T(1,128)}, u32[]{:S(2)}) copy-start(f32[1,64]{1,0:T(1,128)} %get-tuple-element.12) | copy-start | bytes 772
  52.2 0.9 %copy-start.2 = (f32[1,128]{1,0:T(1,128)S(1)}, f32[1,128]{1,0:T(1,128)}, u32[]{:S(2)}) copy-start(f32[1,128]{1,0:T(1,128)} %get-tuple-element.14) | copy-start | bytes 1540

commit v2 on v1

--- a/solution.py
+++ b/solution.py
@@ -171,14 +171,14 @@
 
 
 def kernel(
-    n, m, scale_one, scale_two, each1, each2,
+    n, m, each1, each2,
     act, w1, b1, w2, b2, cot,
-    gin, gw1, gb1, gw2, gb2,
+    gin, s1out, s2out,
     xr, x2, pre1, pool, p2, pre2, cotr, d2, d2t, gp, d1, d1t, gx,
     k1, k2, g1, g2, b1s, b2s, gb1s, gb2s, fold1,
     acth, poolh, gps, gpr, gxs, gxr,
-    s2x, s2got, s2part, s2gots, s2out, s2acc,
-    s1x, s1got, s1part, s1gots, s1out, s1acc,
+    s2x, s2got, s2part, s2gots, s2acc,
+    s1x, s1got, s1part, s1gots, s1acc,
     hsend, hrecv, dsend2, drecv2, zsend2, zrecv2, dsend1, drecv1, zsend1, zrecv1,
 ):
     me = lax.axis_index("dp")
@@ -563,10 +563,14 @@
         for g in range(wide):
             gin[0, d, :, g * 128 : (g + 1) * 128] = xr[pl.ds(g, side, stride=wide), :].astype(BF16)
     sum2.step5()
+    sum1.step5()
+
+
+def unpack(scale_one, scale_two, gin, s1out, s2out, gin_out, gw1, gb1, gw2, gb2):
+    gin_out[...] = gin[...]
     for t in range(9):
         gw2[t] = s2out[t * 192 : (t + 1) * 192, :].astype(F32) * scale_two
     gb2[...] = s2out[1728:1744, :].astype(F32)[0:1, :] * scale_two
-    sum1.step5()
     for t in range(9):
         block = s1out[(t % 5) * 96 : (t % 5) * 96 + 96, :].astype(F32) * scale_one
         gw1[t] = block[:, (t // 5) * 64 : (t // 5) * 64 + 64]
@@ -592,23 +596,20 @@
             vmem((n, m * size, 128), BF16),
             vmem((m * size, 128), BF16),
             vmem((m, slots * size, 128), BF16),
-            vmem((n * m * size, 128), BF16),
             vmem((m * size, 128), F32),
         ]
 
     dma = pltpu.SemaphoreType.DMA
     spec = pl.BlockSpec(memory_space=pltpu.VMEM)
-    outs = pl.pallas_call(
-        functools.partial(kernel, n, m, scale_one, scale_two, each[0], each[1]),
+    sent = pl.pallas_call(
+        functools.partial(kernel, n, m, each[0], each[1]),
         out_shape=[
             jax.ShapeDtypeStruct(act_in.shape, BF16),
-            jax.ShapeDtypeStruct((9, 3 * chan_in, chan_mid), F32),
-            jax.ShapeDtypeStruct((1, chan_mid), F32),
-            jax.ShapeDtypeStruct((9, 3 * chan_mid, chan_out), F32),
-            jax.ShapeDtypeStruct((1, chan_out), F32),
+            jax.ShapeDtypeStruct((n * m * each[0], 128), BF16),
+            jax.ShapeDtypeStruct((n * m * each[1], 128), BF16),
         ],
         in_specs=[spec] * 6,
-        out_specs=[spec] * 5,
+        out_specs=[spec] * 3,
         scratch_shapes=[
             vmem((rows, 128), F32),
             vmem((slab + 2, rows + 2 * wide, 256), BF16),
@@ -662,6 +663,18 @@
         bias_two.reshape(1, chan_out),
         cotangent,
     )
+    outs = pl.pallas_call(
+        functools.partial(unpack, scale_one, scale_two),
+        out_shape=[
+            jax.ShapeDtypeStruct(act_in.shape, BF16),
+            jax.ShapeDtypeStruct((9, 3 * chan_in, chan_mid), F32),
+            jax.ShapeDtypeStruct((1, chan_mid), F32),
+            jax.ShapeDtypeStruct((9, 3 * chan_mid, chan_out), F32),
+            jax.ShapeDtypeStruct((1, chan_out), F32),
+        ],
+        in_specs=[spec] * 3,
+        out_specs=[spec] * 5,
+    )(*sent)
     return (
         outs[0],
         outs[1].reshape(weight_one.shape),

time: 53.8 us -> 51.5 us (0.957)
  local copies, waits for them, and re-layouts: 4.7 us -> 0 us
  Pallas kernels: 48.3 us -> 50.7 us
    unnamed x13 -> x0, local copies, waits for them, and re-layouts: 4.7 us -> none
    pallas_call x1 -> x2, Pallas kernels: 48.3 us -> 50.7 us  [the longest x1 48 us: local(): pl.pallas_call(functools.partial(kernel, n, m, each[0], each[1]), out_sha...]
where the time goes in v2:
time: 51.5 us; the launch traced here: 51.3 us
  Pallas kernels  50.7 us (98%)
  between operations  0.64 us (1%)
    pallas_call x1, Pallas kernels, local(): pl.pallas_call(functools.partial(kernel, n, m, each[0], each[1]), out_sha...  48 us
    pallas_call x1, Pallas kernels, local(): pl.pallas_call(functools.partial(unpack, scale_one, scale_two), out_shape...  2.62 us

profile of v2, /device:TPU:0, one launch (start us, length us, event | category | flops | bytes accessed | tf_op | source)
XLA Modules:
  0.0 51.3 jit_solution(16112432429331617360)
XLA Ops:
  0.6 48.0 %shard_map.101 = (bf16[1,2,64,2048]{3,2,1,0:T(8,128)(2,1)}, bf16[512,128]{1,0:T(8,128)(2,1)}, bf16[2048,128]{1,0:T(8,128)(2,1)}) custom-call(bf16[1,2,64,2048]{3,2,1,0:T(8,128)(2,1)} %act.1, bf16[27,32,64]{2,1,0:T(8,128)(2,1)} %bitcast.9, f32[1,64]{1,0:T(1,128)} %bitcast.10, bf16[27,64,128]{2,1,0:T(8,128)(2,1)} %bitcast.8, f32[1,128]{1,0:T(1,128)} %bitcast.11, ...), custom_call_target="tpu_custom_call" | custom-call | tf_op jit(solution)/shard_map/pallas_call | solution.py:604
  48.7 2.6 %shard_map.102 = (bf16[1,2,64,2048]{3,2,1,0:T(8,128)(2,1)}, f32[9,96,64]{2,1,0:T(8,128)}, f32[1,64]{1,0:T(1,128)}, f32[9,192,128]{2,1,0:T(8,128)}, f32[1,128]{1,0:T(1,128)}) custom-call(bf16[1,2,64,2048]{3,2,1,0:T(8,128)(2,1)} %get-tuple-element.13.gin, bf16[512,128]{1,0:T(8,128)(2,1)} %get-tuple-element.14.s1out, bf16[2048,128]{1,0:T(8,128)(2,1)} %get-tuple-element.15.s2out), custom_call_target="tpu_custom_call" | custom-call | tf_op jit(solution)/shard_map/pallas_call | solution.py:666
